TPU v7x, 32 devices: a whole 2x2x4 slice. The times are simulated.
32 devices in a mesh: face: 8 (over z, core), sub: 4 (over y, x).
Axes of the slice: x: 2, y: 2, z: 4, core: 2. Of those that a mesh axis runs over, the one named last changes fastest.
Arguments:
- mesh_latent: bfloat16 [8192, 512], P(('face', 'sub')), may hold values from -6 to 6
- edge_latent: bfloat16 [65536, 512], P(('face', 'sub')), may hold values from -6 to 6
- grid_features: bfloat16 [8192, 384], P(('face', 'sub')), may hold values from -6 to 6
- senders: int32 [65536], P(('face', 'sub')), may hold values from 0 to 383, as said below
- receivers: int32 [65536], P(('face', 'sub')), may hold values from 0 to 255
- send_lists: int32 [32, 4, 32], P(('face', 'sub')), may hold values from -1 to 255, as said below
- link_sources: int32 [16384], P(('face', 'sub')), may hold values from 0 to 255
- link_targets: int32 [16384], P(('face', 'sub')), may hold values from 0 to 255
- node_area: float32 [8192], P(('face', 'sub')), may hold values from 0.25 to 4.5
- grid_weight: bfloat16 [384, 512], P(None, 'sub'), may hold values from -0.3125 to 0.3125
- encode_weight: bfloat16 [1024, 512], P('sub'), may hold values from -0.1875 to 0.1875
- edge_first: bfloat16 [1, 1536, 512], P(None, 'sub'), may hold values from -0.15625 to 0.15625
- edge_second: bfloat16 [1, 512, 512], P(None, 'sub'), may hold values from -0.25 to 0.25
- node_first: bfloat16 [1, 1024, 512], P(None, 'sub'), may hold values from -0.1875 to 0.1875
- node_second: bfloat16 [1, 512, 512], P(None, 'sub'), may hold values from -0.25 to 0.25
Outputs:
- mesh_result: bfloat16 [8192, 512], P(('face', 'sub'))
- edge_result: bfloat16 [65536, 512], P(('face', 'sub'))
- masses: float32 [1, 512], replicated
Inputs may be any that keep to these rules, and one draw needn't show every extreme that they name: `send_lists`: entries are the sending partition's own node numbers, or -1 for an unused slot; in every list the used slots come first, hold distinct nodes and number 32 // 2 or more; for every list number some partition uses all 32 slots. `senders`: A value below 256 names one of the partition's own nodes; 256 + d * 32 + k names slot k of the list with number d that the partition receives, and that slot is always a used one.
All inputs are finite; a program needn't handle non-finite values.
Results may differ from a plain program's by a relative error of at most 0.008.
Values may be sent and summed in bfloat16 or wider, within the bound.
A program may use at most 64 MiB of HBM per device.

v0:
```python
import jax
import jax.numpy as jnp
from jax import lax
from jax.sharding import PartitionSpec as P


def passed_along(value, axis, steps):
    count = lax.axis_size(axis)
    pairs = [(source, (source + steps) % count) for source in range(count)]
    return lax.ppermute(value, axis, pairs)


def fold_rows(weight, operand):
    return jnp.dot(
        operand,
        lax.all_gather(weight, "sub", axis=0, tiled=True),
        preferred_element_type=jnp.float32,
    )


def edge_rows(weight, operand):
    storage = jnp.zeros((1, weight.shape[1]), jnp.bfloat16)
    total = jnp.dot(
        operand,
        lax.all_gather(weight, "sub", axis=0, tiled=True),
        preferred_element_type=jnp.float32,
    )
    return (total, storage)


def along_face(values, offset):
    return passed_along(values, "face", offset)


def along_sub(values, offset):
    return passed_along(values, "sub", offset)


def per_device(
    mesh_latent,
    edge_latent,
    grid_features,
    senders,
    receivers,
    send_lists,
    link_sources,
    link_targets,
    node_area,
    grid_weight,
    encode_weight,
    edge_first,
    edge_second,
    node_first,
    node_second,
):
    node_rows = mesh_latent.shape[0]
    nodes_all = node_rows * lax.axis_size("face") * lax.axis_size("sub")
    grid_latent = jax.nn.silu(
        jnp.dot(
            grid_features,
            lax.all_gather(grid_weight, "sub", axis=1, tiled=True),
            preferred_element_type=jnp.float32,
        )
    ).astype(jnp.bfloat16)

    def project(weight, operand):
        return fold_rows(weight, operand)

    node_ids = jnp.arange(node_rows, dtype=jnp.int32)
    joined = jnp.concatenate(
        [jnp.take(grid_latent, link_sources, axis=0), jnp.take(mesh_latent, link_targets, axis=0)],
        axis=1,
    )
    messages = jax.nn.silu(project(encode_weight, joined)).astype(jnp.bfloat16)
    target_onehot = (link_targets[:, None] == node_ids[None, :]).astype(jnp.bfloat16)
    arriving = lax.dot_general(
        target_onehot, messages, (((0,), (0,)), ((), ())), preferred_element_type=jnp.float32
    )
    latent = (mesh_latent.astype(jnp.float32) + arriving).astype(jnp.bfloat16)
    halo_lists = send_lists[0]
    list_mask = (halo_lists >= 0)[:, :, None]
    receive_onehot = (receivers[:, None] == node_ids[None, :]).astype(jnp.bfloat16)
    edge_state = edge_latent
    picked = jnp.take(latent, jnp.maximum(halo_lists, 0), axis=0)
    picked = jnp.where(list_mask, picked, jnp.zeros((), jnp.bfloat16))
    lower_face = along_face(picked[0], 1)
    upper_face = along_face(picked[1], -1)
    lower_sub = along_sub(picked[2], 1)
    upper_sub = along_sub(picked[3], -1)
    arrived = jnp.concatenate([lower_face, upper_face, lower_sub, upper_sub], axis=0)
    receiving_rows = jnp.take(latent, receivers, axis=0)
    node_table = jnp.concatenate([latent, arrived], axis=0)
    inputs = jnp.concatenate(
        [edge_state, jnp.take(node_table, senders, axis=0), receiving_rows], axis=1
    )
    before, unused_rows = edge_rows(edge_first[0], inputs)
    hidden = jax.nn.silu(before).astype(jnp.bfloat16)
    edge_state = (edge_state.astype(jnp.float32) + project(edge_second[0], hidden)).astype(
        jnp.bfloat16
    )
    incoming = lax.dot_general(
        receive_onehot, edge_state, (((0,), (0,)), ((), ())), preferred_element_type=jnp.float32
    ).astype(jnp.bfloat16)
    node_hidden = jax.nn.silu(
        project(node_first[0], jnp.concatenate([latent, incoming], axis=1))
    ).astype(jnp.bfloat16)
    latent = (latent.astype(jnp.float32) + project(node_second[0], node_hidden)).astype(
        jnp.bfloat16
    )
    totals = [jnp.dot(node_area, latent.astype(jnp.float32), precision=lax.Precision.HIGHEST)]
    stacked = lax.psum(jnp.stack(totals), ("face", "sub"))
    masses = stacked / nodes_all
    return (latent, edge_state, masses)


def solution(mesh):
    in_specs = (
        P(("face", "sub"), None),
        P(("face", "sub"), None),
        P(("face", "sub"), None),
        P(("face", "sub")),
        P(("face", "sub")),
        P(("face", "sub"), None, None),
        P(("face", "sub")),
        P(("face", "sub")),
        P(("face", "sub")),
        P(None, "sub"),
        P("sub", None),
        P(None, "sub", None),
        P(None, "sub", None),
        P(None, "sub", None),
        P(None, "sub", None),
    )
    out_specs = (P(("face", "sub"), None), P(("face", "sub"), None), P())
    return jax.shard_map(
        per_device, mesh=mesh, in_specs=in_specs, out_specs=out_specs, check_vma=False
    )
```

profile of v0, /device:TPU:0, one launch (start us, length us, event | category | flops | bytes accessed | tf_op | source)
XLA Modules:
  0.0 153.9 jit_solution(15797503033091889898)
XLA Ops:
  7.2 0.0 copy-start
  7.2 0.0 copy-start.3
  7.2 0.0 all-gather.8.cloned.1.call-start
  7.2 0.7 all-gather.8.cloned.1.call-update
  7.9 0.0 all-gather.10.cloned.1.call-start
  8.0 0.7 all-gather.10.cloned.1.call-update
  8.7 0.0 all-gather.12.cloned.1.call-start
  8.7 0.7 all-gather.12.cloned.1.call-update
  9.4 0.7 compare_select_fusion.2
  10.1 0.7 compare_and_fusion.2
  10.8 0.7 compare_select_fusion.3
  11.5 0.7 compare_and_fusion.3
  12.2 0.7 broadcast_maximum_fusion
  12.8 0.7 compare_bitcast_fusion.1
  13.5 0.7 fusion.46
  14.2 1.3 compare_and_fusion.1
  15.5 0.7 fusion.47
  16.2 1.3 compare_and_fusion
  17.5 12.5 %all_gather.18 = bf16[384,512]{1,0:T(8,128)(2,1)S(1)} all-gather(bf16[384,128]{1,0:T(8,128)(2,1)} %param.26), channel_id=1, replica_groups=mesh['face'=8,'sub'=4] {'sub'}, dimensions={1}, use_global_device_ids=true | all-gather | bytes 491520 | tf_op jit(solution)/shard_map/all_gather | solution.py:61
  30.1 0.1 reshape.70
  30.1 13.3 %all-gather.1 = bf16[1,512,512]{2,1,0:T(8,128)(2,1)} all-gather(bf16[1,128,512]{2,1,0:T(8,128)(2,1)} %param.29), channel_id=3, replica_groups=mesh['face'=8,'sub'=4] {'sub'}, dimensions={1}, use_global_device_ids=true | all-gather | bytes 655360 | tf_op jit(solution)/shard_map/all_gather | solution.py:16
  43.5 0.0 copy-done.3
  43.5 10.7 %all-gather.3 = bf16[1,512,512]{2,1,0:T(8,128)(2,1)S(1)} all-gather(bf16[1,128,512]{2,1,0:T(8,128)(2,1)S(1)} %copy-done.3), channel_id=5, replica_groups=mesh['face'=8,'sub'=4] {'sub'}, dimensions={1}, use_global_device_ids=true | all-gather | bytes 655360 | tf_op jit(solution)/shard_map/all_gather | solution.py:16
  54.2 0.0 copy-done
  54.2 0.4 multiply_convert_fusion.4
  54.6 0.0 copy-start.1
  54.6 2.0 %gather_fusion.3 = bf16[512,512]{1,0:T(8,128)(2,1)S(1)} fusion(bf16[256,512]{1,0:T(8,128)(2,1)S(1)} %multiply_convert_fusion.4, s32[1024]{0:T(1024)S(1)} %pad_clamp_fusion.2), kind=kCustom, calls=%fused_computation.clone | custom fusion | bytes 1050624 | tf_op jit(solution)/shard_map/jit(_take)/gather | solution.py:71
  56.5 0.0 copy-done.1
  56.6 2.0 %gather_fusion.4 = bf16[512,512]{1,0:T(8,128)(2,1)S(1)} fusion(bf16[256,512]{1,0:T(8,128)(2,1)S(1)} %copy-done.1, s32[1024]{0:T(1024)S(1)} %pad_clamp_fusion.1), kind=kCustom, calls=%fused_computation.1.clone | custom fusion | bytes 1050624 | tf_op jit(solution)/shard_map/jit(_take)/gather | solution.py:71
  58.5 0.0 copy-start.6
  58.5 0.2 broadcast_select_fusion.2
  58.8 0.0 all-gather.8.cloned.1.call-done
  58.8 0.4 copy-done.6
  59.2 2.3 %constant_dynamic-update-slice_fusion.4 = (bf16[384,512]{1,0:T(8,128)(2,1)S(1)}, bf16[256,512]{1,0:T(8,128)(2,1)S(1)}) fusion(bf16[1024,512]{1,0:T(8,128)(2,1)} %all-gather.8.cloned.1.call-done, bf16[512,512]{1,0:T(8,128)(2,1)S(1)} %get-tuple-element.12, bf16[512,512]{1,0:T(8,128)(2,1)S(1)} %get-tuple-element.13, s32[512]{0:T(512)S(1)} %copy-done.6, ...), kind=kOutput, calls=%fused_computation.55 | convolution fusion | flops 675020800 | bytes 2885632 | tf_op jit(solution)/shard_map/dot_general | solution.py:76
  61.5 0.8 gather_fusion
  62.4 0.1 select_select_fusion
  62.5 0.6 slice_bitcast_fusion
  63.1 0.0 collective-permute-start
  63.1 3.5 %collective-permute-start.1 = (bf16[32,512]{1,0:T(8,128)(2,1)}, bf16[32,512]{1,0:T(8,128)(2,1)}, u32[]{:S(2)}, u32[]{:S(2)}) collective-permute-start(bf16[32,512]{1,0:T(8,128)(2,1)} %get-tuple-element.6), channel_id=1, source_target_pairs={{0,28},{4,0},{8,4},{12,8},{16,12},{20,16},{24,20},{28,24},{1,29},{... | collective-permute-start | bytes 98312 | tf_op jit(solution)/shard_map/ppermute | solution.py:10
  66.7 0.4 collective-permute-start.2
  67.1 2.5 %collective-permute-start.3 = (bf16[32,512]{1,0:T(8,128)(2,1)}, bf16[32,512]{1,0:T(8,128)(2,1)S(1)}, u32[]{:S(2)}, u32[]{:S(2)}) collective-permute-start(bf16[32,512]{1,0:T(8,128)(2,1)} %get-tuple-element.4), channel_id=1, source_target_pairs={{0,3},{1,0},{2,1},{3,2},{4,7},{5,4},{6,5},{7,6},{8,11},{9,8},{10,9... | collective-permute-start | bytes 98312 | tf_op jit(solution)/shard_map/ppermute | solution.py:10
  69.6 7.5 %gather_fusion.2 = bf16[2048,512]{1,0:T(8,128)(2,1)S(1)} fusion(bf16[256,512]{1,0:T(8,128)(2,1)S(1)} %get-tuple-element.11, s32[2048]{0:T(1024)S(1)} %fusion.47), kind=kCustom, calls=%fused_computation.4 | custom fusion | bytes 4202496 | tf_op jit(solution)/shard_map/jit(_take)/gather | solution.py:91
  77.1 2.2 %broadcast_select_fusion = bf16[2048,512]{1,0:T(8,128)(2,1)} fusion(bf16[2048,512]{1,0:T(8,128)(2,1)S(1)} %gather_fusion.2, pred[2048]{0:T(1024)(128)(4,1)} %compare_and_fusion), kind=kLoop, calls=%fused_computation.14 | loop fusion | flops 1048576 | bytes 4196352 | tf_op jit(solution)/shard_map/jit(_take)/select_n | solution.py:91
  79.4 0.0 collective-permute-done
  79.4 0.8 constant_dynamic-update-slice_fusion.3
  80.1 0.0 collective-permute-done.1
  80.1 0.8 constant_dynamic-update-slice_fusion.2
  80.9 0.0 collective-permute-done.2
  80.9 0.0 collective-permute-done.3
  80.9 0.0 copy-start.5
  80.9 7.5 %gather_fusion.1 = bf16[2048,512]{1,0:T(8,128)(2,1)S(1)} fusion(bf16[384,512]{1,0:T(8,128)(2,1)S(1)} %constant_dynamic-update-slice_fusion, s32[2048]{0:T(1024)S(1)} %fusion.46), kind=kCustom, calls=%fused_computation.3 | custom fusion | bytes 4202496 | tf_op jit(solution)/shard_map/jit(_take)/gather | solution.py:94
  88.5 0.0 copy-done.5
  88.5 1.6 %broadcast_select_fusion.1 = bf16[2048,512]{1,0:T(8,128)(2,1)} fusion(bf16[2048,512]{1,0:T(8,128)(2,1)S(1)} %gather_fusion.1, pred[2048]{0:T(1024)(128)(4,1)S(1)} %copy-done.5), kind=kLoop, calls=%fused_computation.15 | loop fusion | flops 1048576 | bytes 4196352 | tf_op jit(solution)/shard_map/jit(_take)/select_n | solution.py:94
  90.0 8.5 %add_convert_fusion = bf16[2048,512]{1,0:T(8,128)(2,1)S(1)} fusion(bf16[2048,512]{1,0:T(8,128)(2,1)} %param.18, bf16[2048,512]{1,0:T(8,128)(2,1)} %broadcast_select_fusion, bf16[2048,512]{1,0:T(8,128)(2,1)} %broadcast_select_fusion.1, bf16[1,1536,512]{2,1,0:T(8,128)(2,1)} %all-gather.10.cloned.1.call-done, bf16[1,512,512]{2,1,0:T(8,128)(2,1)} %all-gather.1), kind=kOutput, calls=%fused_computation.11 | convolution fusion | flops 4322230272 | bytes 10485760 | tf_op jit(solution)/shard_map/dot_general | solution.py:14
  98.6 0.0 copy-done.4
  98.6 0.0 copy-start.8
  98.6 1.8 %fusion.8 = bf16[256,512]{1,0:T(8,128)(2,1)} fusion(bf16[2048,512]{1,0:T(8,128)(2,1)S(1)} %add_convert_fusion, s32[2048]{0:T(1024)S(1)} %copy-done.4), kind=kOutput, calls=%fused_computation.20 | convolution fusion | flops 537526272 | bytes 2367488 | tf_op jit(solution)/shard_map/dot_general | solution.py:101
  100.4 4.8 %all-gather.12.cloned.1.call-done = bf16[1,1024,512]{2,1,0:T(8,128)(2,1)} async-done(((bf16[1,256,512]{2,1,0:T(8,128)(2,1)}), bf16[1,1024,512]{2,1,0:T(8,128)(2,1)}) %all-gather.12.cloned.1.call-update) | async-done | bytes 1048592 | tf_op jit(solution)/shard_map/all_gather | solution.py:16
  105.3 2.0 %fusion.10 = bf16[256,512]{1,0:T(8,128)(2,1)S(1)} fusion(bf16[1,512,512]{2,1,0:T(8,128)(2,1)S(1)} %all-gather.3, bf16[1,1024,512]{2,1,0:T(8,128)(2,1)} %all-gather.12.cloned.1.call-done, bf16[256,512]{1,0:T(8,128)(2,1)} %fusion.8, bf16[256,512]{1,0:T(8,128)(2,1)S(1)} %get-tuple-element.11), kind=kOutput, calls=%fused_computation.22 | convolution fusion | flops 404750336 | bytes 2359296 | tf_op jit(solution)/shard_map/dot_general | solution.py:14
  107.3 0.0 copy-done.8
  107.3 0.0 copy-start.2
  107.3 0.2 fusion.59
  107.5 39.2 %psum.7 = f32[1,512]{1,0:T(1,128)S(1)} all-reduce(f32[1,512]{1,0:T(1,128)S(1)} %fusion.59), channel_id=1, replica_groups=mesh['face'=8,'sub'=4] {'face','sub'}, use_global_device_ids=true, to_apply=%region_0.2 | all-reduce | flops 512 | bytes 4096 | tf_op jit(solution)/shard_map/psum | solution.py:111
  146.8 0.6 broadcast_multiply_fusion
  (10 shorter events, 0.0 us)
Async XLA Ops:
  7.2 47.0 %copy-start = (bf16[256,384]{1,0:T(8,128)(2,1)S(1)}, bf16[256,384]{1,0:T(8,128)(2,1)}, u32[]{:S(2)}) copy-start(bf16[256,384]{1,0:T(8,128)(2,1)} %param.19) | copy-start | bytes 589828
  7.2 36.3 %copy-start.3 = (bf16[1,128,512]{2,1,0:T(8,128)(2,1)S(1)}, bf16[1,128,512]{2,1,0:T(8,128)(2,1)}, u32[]{:S(2)}) copy-start(bf16[1,128,512]{2,1,0:T(8,128)(2,1)} %param.31) | copy-start | bytes 393220
  7.2 51.6 %all-gather.8.cloned.1.call-start = ((), (), s32[]{:S(2)}) async-start(), calls=%async_computation | async-start | bytes 1310720 | tf_op jit(solution)/shard_map/all_gather | solution.py:16
  7.9 82.1 %all-gather.10.cloned.1.call-start = ((), (), s32[]{:S(2)}) async-start(), calls=%async_computation.1 | async-start | bytes 1966080 | tf_op jit(solution)/shard_map/all_gather | solution.py:25
  8.7 96.6 %all-gather.12.cloned.1.call-start = ((), (), s32[]{:S(2)}) async-start(), calls=%async_computation.2 | async-start | bytes 1310720 | tf_op jit(solution)/shard_map/all_gather | solution.py:16
  54.6 2.0 %copy-start.1 = (bf16[256,512]{1,0:T(8,128)(2,1)S(1)}, bf16[256,512]{1,0:T(8,128)(2,1)}, u32[]{:S(2)}) copy-start(bf16[256,512]{1,0:T(8,128)(2,1)} %param.17) | copy-start | bytes 786436
  58.5 0.7 copy-start.6
  63.1 16.2 %collective-permute-start = (bf16[32,512]{1,0:T(8,128)(2,1)}, bf16[32,512]{1,0:T(8,128)(2,1)}, u32[]{:S(2)}, u32[]{:S(2)}) collective-permute-start(bf16[32,512]{1,0:T(8,128)(2,1)} %get-tuple-element.7), channel_id=1, source_target_pairs={{0,4},{4,8},{8,12},{12,16},{16,20},{20,24},{24,28},{28,0},{1,5},{5... | collective-permute-start | bytes 98312 | tf_op jit(solution)/shard_map/ppermute | solution.py:10
  63.1 17.0 %collective-permute-start.1 = (bf16[32,512]{1,0:T(8,128)(2,1)}, bf16[32,512]{1,0:T(8,128)(2,1)}, u32[]{:S(2)}, u32[]{:S(2)}) collective-permute-start(bf16[32,512]{1,0:T(8,128)(2,1)} %get-tuple-element.6), channel_id=1, source_target_pairs={{0,28},{4,0},{8,4},{12,8},{16,12},{20,16},{24,20},{28,24},{1,29},{... | collective-permute-start | bytes 98312 | tf_op jit(solution)/shard_map/ppermute | solution.py:10
  66.7 14.2 %collective-permute-start.2 = (bf16[32,512]{1,0:T(8,128)(2,1)}, bf16[32,512]{1,0:T(8,128)(2,1)S(1)}, u32[]{:S(2)}, u32[]{:S(2)}) collective-permute-start(bf16[32,512]{1,0:T(8,128)(2,1)} %get-tuple-element.5), channel_id=1, source_target_pairs={{0,1},{1,2},{2,3},{3,0},{4,5},{5,6},{6,7},{7,4},{8,9},{9,10},{10,1... | collective-permute-start | bytes 98312 | tf_op jit(solution)/shard_map/ppermute | solution.py:10
  67.1 13.8 %collective-permute-start.3 = (bf16[32,512]{1,0:T(8,128)(2,1)}, bf16[32,512]{1,0:T(8,128)(2,1)S(1)}, u32[]{:S(2)}, u32[]{:S(2)}) collective-permute-start(bf16[32,512]{1,0:T(8,128)(2,1)} %get-tuple-element.4), channel_id=1, source_target_pairs={{0,3},{1,0},{2,1},{3,2},{4,7},{5,4},{6,5},{7,6},{8,11},{9,8},{10,9... | collective-permute-start | bytes 98312 | tf_op jit(solution)/shard_map/ppermute | solution.py:10
  80.9 7.6 %copy-start.5 = (pred[2048]{0:T(1024)(128)(4,1)S(1)}, pred[2048]{0:T(1024)(128)(4,1)}, u32[]{:S(2)}) copy-start(pred[2048]{0:T(1024)(128)(4,1)} %compare_and_fusion.1) | copy-start | bytes 6148
  90.0 8.5 %copy-start.4 = (s32[2048]{0:T(1024)S(1)}, s32[2048]{0:T(1024)}, u32[]{:S(2)}) copy-start(s32[2048]{0:T(1024)} %param.21) | copy-start | bytes 24580
  98.6 8.7 %copy-start.8 = (bf16[2048,512]{1,0:T(8,128)(2,1)}, bf16[2048,512]{1,0:T(8,128)(2,1)S(1)}, u32[]{:S(2)}) copy-start(bf16[2048,512]{1,0:T(8,128)(2,1)S(1)} %add_convert_fusion) | copy-start | bytes 6291460
  100.4 6.9 %copy-start.7 = (f32[256]{0:T(256)S(1)}, f32[256]{0:T(256)}, u32[]{:S(2)}) copy-start(f32[256]{0:T(256)} %param.25) | copy-start | bytes 3076
  107.3 40.1 %copy-start.2 = (bf16[256,512]{1,0:T(8,128)(2,1)}, bf16[256,512]{1,0:T(8,128)(2,1)S(1)}, u32[]{:S(2)}) copy-start(bf16[256,512]{1,0:T(8,128)(2,1)S(1)} %fusion.10) | copy-start | bytes 786436
Sparse Core Ops, SparseCore 0:
  9.8 32.7 all-gather.7
  44.4 32.7 all-gather.9
  79.1 26.1 all-gather.11
where the time goes:
time: 155 us; the launch traced here: 154 us
  blocking collectives  75.8 us (49%)
  local copies, waits for them, and re-layouts  22.6 us (15%)
  matrix products  15.3 us (10%)
  between operations  14 us (9%)
  other arithmetic  12.7 us (8%)
  waiting for transfers between devices  6.92 us (4%)
  starting transfers between devices  6.58 us (4%)
    psum x1, blocking collectives, per_device(): stacked = lax.psum(jnp.stack(totals), ('face', 'sub'))  39.2 us
    all_gather x2, blocking collectives, fold_rows(): lax.all_gather(weight, 'sub', axis=0, tiled=True)  24 us
    all_gather x1, blocking collectives, per_device(): lax.all_gather(grid_weight, 'sub', axis=1, tiled=True)  12.5 us
    dot_general x2, matrix products, fold_rows(): jnp.dot(operand, lax.all_gather(weight, 'sub', axis=0, tiled=True), prefe...  10.5 us
    gather x1, local copies, waits for them, and re-layouts, per_device(): jnp.take(node_table, senders, axis=0)  7.54 us
    gather x1, local copies, waits for them, and re-layouts, per_device(): receiving_rows = jnp.take(latent, receivers, axis=0)  7.53 us
    ppermute x4, starting transfers between devices, passed_along(): return lax.ppermute(value, axis, pairs)  6.47 us
    all_gather x2, waiting for transfers between devices, fold_rows(): lax.all_gather(weight, 'sub', axis=0, tiled=True)  4.85 us
  transfers between devices with their start and end apart: 7, of which 1 were waited for; matrix products, arithmetic and copies ran while one was open for 31% of the time, Pallas kernels for 0%

commit v1 on v0

--- a/solution.py
+++ b/solution.py
@@ -108,7 +108,8 @@
         jnp.bfloat16
     )
     totals = [jnp.dot(node_area, latent.astype(jnp.float32), precision=lax.Precision.HIGHEST)]
-    stacked = lax.psum(jnp.stack(totals), ("face", "sub"))
+    one_axis = lax.psum(jnp.stack(totals), "sub")
+    stacked = lax.psum(one_axis, "face")
     masses = stacked / nodes_all
     return (latent, edge_state, masses)
 

time: 155 us -> 139 us (0.90)
  blocking collectives: 75.8 us -> 59.6 us
    psum x1 -> x2, blocking collectives: 39.2 us -> 23.1 us  [the longest x1 14.1 us: per_device(): stacked = lax.psum(one_axis, 'face')]
  transfers between devices with their start and end apart: 7 -> 7, of which waited for: 1 -> 1; matrix products, arithmetic and copies ran while one was open for 31% -> 34% of each run, Pallas kernels for 0% -> 0%
where the time goes in v1:
time: 139 us; the launch traced here: 138 us
  blocking collectives  59.6 us (43%)
  local copies, waits for them, and re-layouts  22.6 us (16%)
  matrix products  15.3 us (11%)
  between operations  14 us (10%)
  other arithmetic  12.8 us (9%)
  waiting for transfers between devices  6.83 us (5%)
  starting transfers between devices  6.58 us (5%)
    all_gather x2, blocking collectives, fold_rows(): lax.all_gather(weight, 'sub', axis=0, tiled=True)  24 us
    psum x1, blocking collectives, per_device(): stacked = lax.psum(one_axis, 'face')  14.1 us
    all_gather x1, blocking collectives, per_device(): lax.all_gather(grid_weight, 'sub', axis=1, tiled=True)  12.5 us
    dot_general x2, matrix products, fold_rows(): jnp.dot(operand, lax.all_gather(weight, 'sub', axis=0, tiled=True), prefe...  10.6 us
    psum x1, blocking collectives, per_device(): one_axis = lax.psum(jnp.stack(totals), 'sub')  8.92 us
    gather x1, local copies, waits for them, and re-layouts, per_device(): jnp.take(node_table, senders, axis=0)  7.54 us
    gather x1, local copies, waits for them, and re-layouts, per_device(): receiving_rows = jnp.take(latent, receivers, axis=0)  7.53 us
    ppermute x4, starting transfers between devices, passed_along(): return lax.ppermute(value, axis, pairs)  6.47 us
  transfers between devices with their start and end apart: 7, of which 1 were waited for; matrix products, arithmetic and copies ran while one was open for 34% of the time, Pallas kernels for 0%

profile of v1, /device:TPU:0, one launch (start us, length us, event | category | flops | bytes accessed | tf_op | source)
XLA Modules:
  0.0 137.7 jit_solution(8272117815122790294)
XLA Ops:
  7.2 0.0 copy-start
  7.2 0.0 copy-start.3
  7.2 0.0 all-gather.8.cloned.1.call-start
  7.2 0.7 all-gather.8.cloned.1.call-update
  7.9 0.0 all-gather.10.cloned.1.call-start
  8.0 0.7 all-gather.10.cloned.1.call-update
  8.7 0.0 all-gather.12.cloned.1.call-start
  8.7 0.7 all-gather.12.cloned.1.call-update
  9.4 0.7 compare_select_fusion.2
  10.1 0.7 compare_and_fusion.2
  10.8 0.7 compare_select_fusion.3
  11.5 0.7 compare_and_fusion.3
  12.2 0.7 broadcast_maximum_fusion
  12.8 0.7 compare_bitcast_fusion.1
  13.5 0.7 fusion.46
  14.2 1.3 compare_and_fusion.1
  15.5 0.7 fusion.47
  16.2 1.3 compare_and_fusion
  17.5 12.5 %all_gather.18 = bf16[384,512]{1,0:T(8,128)(2,1)S(1)} all-gather(bf16[384,128]{1,0:T(8,128)(2,1)} %param.26), channel_id=1, replica_groups=mesh['face'=8,'sub'=4] {'sub'}, dimensions={1}, use_global_device_ids=true | all-gather | bytes 491520 | tf_op jit(solution)/shard_map/all_gather | solution.py:61
  30.1 0.1 reshape.70
  30.1 13.3 %all-gather.1 = bf16[1,512,512]{2,1,0:T(8,128)(2,1)} all-gather(bf16[1,128,512]{2,1,0:T(8,128)(2,1)} %param.29), channel_id=3, replica_groups=mesh['face'=8,'sub'=4] {'sub'}, dimensions={1}, use_global_device_ids=true | all-gather | bytes 655360 | tf_op jit(solution)/shard_map/all_gather | solution.py:16
  43.5 10.7 %all-gather.3 = bf16[1,512,512]{2,1,0:T(8,128)(2,1)S(1)} all-gather(bf16[1,128,512]{2,1,0:T(8,128)(2,1)S(1)} %copy-done.3), channel_id=5, replica_groups=mesh['face'=8,'sub'=4] {'sub'}, dimensions={1}, use_global_device_ids=true | all-gather | bytes 655360 | tf_op jit(solution)/shard_map/all_gather | solution.py:16
  54.2 0.0 copy-done
  54.2 0.4 multiply_convert_fusion.4
  54.6 0.0 copy-start.1
  54.6 2.0 %gather_fusion.3 = bf16[512,512]{1,0:T(8,128)(2,1)S(1)} fusion(bf16[256,512]{1,0:T(8,128)(2,1)S(1)} %multiply_convert_fusion.4, s32[1024]{0:T(1024)S(1)} %pad_clamp_fusion.2), kind=kCustom, calls=%fused_computation.clone | custom fusion | bytes 1050624 | tf_op jit(solution)/shard_map/jit(_take)/gather | solution.py:71
  56.5 0.0 copy-done.1
  56.6 2.0 %gather_fusion.4 = bf16[512,512]{1,0:T(8,128)(2,1)S(1)} fusion(bf16[256,512]{1,0:T(8,128)(2,1)S(1)} %copy-done.1, s32[1024]{0:T(1024)S(1)} %pad_clamp_fusion.1), kind=kCustom, calls=%fused_computation.1.clone | custom fusion | bytes 1050624 | tf_op jit(solution)/shard_map/jit(_take)/gather | solution.py:71
  58.5 0.0 copy-start.6
  58.5 0.2 broadcast_select_fusion.2
  58.8 0.0 all-gather.8.cloned.1.call-done
  58.8 0.4 copy-done.6
  59.2 2.3 %constant_dynamic-update-slice_fusion.4 = (bf16[384,512]{1,0:T(8,128)(2,1)S(1)}, bf16[256,512]{1,0:T(8,128)(2,1)S(1)}) fusion(bf16[1024,512]{1,0:T(8,128)(2,1)} %all-gather.8.cloned.1.call-done, bf16[512,512]{1,0:T(8,128)(2,1)S(1)} %get-tuple-element.12, bf16[512,512]{1,0:T(8,128)(2,1)S(1)} %get-tuple-element.13, s32[512]{0:T(512)S(1)} %copy-done.6, ...), kind=kOutput, calls=%fused_computation.55 | convolution fusion | flops 675020800 | bytes 2885632 | tf_op jit(solution)/shard_map/dot_general | solution.py:76
  61.5 0.8 gather_fusion
  62.4 0.1 select_select_fusion
  62.5 0.7 slice_bitcast_fusion
  63.2 0.0 collective-permute-start
  63.2 3.5 %collective-permute-start.1 = (bf16[32,512]{1,0:T(8,128)(2,1)}, bf16[32,512]{1,0:T(8,128)(2,1)}, u32[]{:S(2)}, u32[]{:S(2)}) collective-permute-start(bf16[32,512]{1,0:T(8,128)(2,1)} %get-tuple-element.6), channel_id=1, source_target_pairs={{0,28},{4,0},{8,4},{12,8},{16,12},{20,16},{24,20},{28,24},{1,29},{... | collective-permute-start | bytes 98312 | tf_op jit(solution)/shard_map/ppermute | solution.py:10
  66.7 0.4 collective-permute-start.2
  67.1 2.5 %collective-permute-start.3 = (bf16[32,512]{1,0:T(8,128)(2,1)}, bf16[32,512]{1,0:T(8,128)(2,1)S(1)}, u32[]{:S(2)}, u32[]{:S(2)}) collective-permute-start(bf16[32,512]{1,0:T(8,128)(2,1)} %get-tuple-element.4), channel_id=1, source_target_pairs={{0,3},{1,0},{2,1},{3,2},{4,7},{5,4},{6,5},{7,6},{8,11},{9,8},{10,9... | collective-permute-start | bytes 98312 | tf_op jit(solution)/shard_map/ppermute | solution.py:10
  69.6 7.5 %gather_fusion.2 = bf16[2048,512]{1,0:T(8,128)(2,1)S(1)} fusion(bf16[256,512]{1,0:T(8,128)(2,1)S(1)} %get-tuple-element.11, s32[2048]{0:T(1024)S(1)} %fusion.47), kind=kCustom, calls=%fused_computation.4 | custom fusion | bytes 4202496 | tf_op jit(solution)/shard_map/jit(_take)/gather | solution.py:91
  77.2 2.2 %broadcast_select_fusion = bf16[2048,512]{1,0:T(8,128)(2,1)} fusion(bf16[2048,512]{1,0:T(8,128)(2,1)S(1)} %gather_fusion.2, pred[2048]{0:T(1024)(128)(4,1)} %compare_and_fusion), kind=kLoop, calls=%fused_computation.14 | loop fusion | flops 1048576 | bytes 4196352 | tf_op jit(solution)/shard_map/jit(_take)/select_n | solution.py:91
  79.4 0.0 collective-permute-done
  79.4 0.8 constant_dynamic-update-slice_fusion.3
  80.1 0.0 collective-permute-done.1
  80.1 0.8 constant_dynamic-update-slice_fusion.2
  80.9 0.0 collective-permute-done.2
  80.9 0.0 collective-permute-done.3
  80.9 0.0 copy-start.5
  81.0 7.5 %gather_fusion.1 = bf16[2048,512]{1,0:T(8,128)(2,1)S(1)} fusion(bf16[384,512]{1,0:T(8,128)(2,1)S(1)} %constant_dynamic-update-slice_fusion, s32[2048]{0:T(1024)S(1)} %fusion.46), kind=kCustom, calls=%fused_computation.3 | custom fusion | bytes 4202496 | tf_op jit(solution)/shard_map/jit(_take)/gather | solution.py:94
  88.5 0.0 copy-done.5
  88.5 1.6 %broadcast_select_fusion.1 = bf16[2048,512]{1,0:T(8,128)(2,1)} fusion(bf16[2048,512]{1,0:T(8,128)(2,1)S(1)} %gather_fusion.1, pred[2048]{0:T(1024)(128)(4,1)S(1)} %copy-done.5), kind=kLoop, calls=%fused_computation.15 | loop fusion | flops 1048576 | bytes 4196352 | tf_op jit(solution)/shard_map/jit(_take)/select_n | solution.py:94
  90.1 8.6 %add_convert_fusion = bf16[2048,512]{1,0:T(8,128)(2,1)S(1)} fusion(bf16[2048,512]{1,0:T(8,128)(2,1)} %param.18, bf16[2048,512]{1,0:T(8,128)(2,1)} %broadcast_select_fusion, bf16[2048,512]{1,0:T(8,128)(2,1)} %broadcast_select_fusion.1, bf16[1,1536,512]{2,1,0:T(8,128)(2,1)} %all-gather.10.cloned.1.call-done, bf16[1,512,512]{2,1,0:T(8,128)(2,1)} %all-gather.1), kind=kOutput, calls=%fused_computation.11 | convolution fusion | flops 4322230272 | bytes 10485760 | tf_op jit(solution)/shard_map/dot_general | solution.py:14
  98.6 0.0 copy-done.4
  98.7 0.0 copy-start.8
  98.7 1.8 %fusion.8 = bf16[256,512]{1,0:T(8,128)(2,1)} fusion(bf16[2048,512]{1,0:T(8,128)(2,1)S(1)} %add_convert_fusion, s32[2048]{0:T(1024)S(1)} %copy-done.4), kind=kOutput, calls=%fused_computation.20 | convolution fusion | flops 537526272 | bytes 2367488 | tf_op jit(solution)/shard_map/dot_general | solution.py:101
  100.5 4.7 %all-gather.12.cloned.1.call-done = bf16[1,1024,512]{2,1,0:T(8,128)(2,1)} async-done(((bf16[1,256,512]{2,1,0:T(8,128)(2,1)}), bf16[1,1024,512]{2,1,0:T(8,128)(2,1)}) %all-gather.12.cloned.1.call-update) | async-done | bytes 1048592 | tf_op jit(solution)/shard_map/all_gather | solution.py:16
  105.2 2.0 %fusion.10 = bf16[256,512]{1,0:T(8,128)(2,1)S(1)} fusion(bf16[1,512,512]{2,1,0:T(8,128)(2,1)S(1)} %all-gather.3, bf16[1,1024,512]{2,1,0:T(8,128)(2,1)} %all-gather.12.cloned.1.call-done, bf16[256,512]{1,0:T(8,128)(2,1)} %fusion.8, bf16[256,512]{1,0:T(8,128)(2,1)S(1)} %get-tuple-element.11), kind=kOutput, calls=%fused_computation.22 | convolution fusion | flops 404750336 | bytes 2359296 | tf_op jit(solution)/shard_map/dot_general | solution.py:14
  107.3 0.0 copy-done.8
  107.3 0.0 copy-start.2
  107.3 0.2 fusion.59
  107.5 8.9 %psum.14 = f32[1,512]{1,0:T(1,128)S(1)} all-reduce(f32[1,512]{1,0:T(1,128)S(1)} %fusion.59), channel_id=1, replica_groups=mesh['face'=8,'sub'=4] {'sub'}, use_global_device_ids=true, to_apply=%region_0.2 | all-reduce | flops 512 | bytes 4096 | tf_op jit(solution)/shard_map/psum | solution.py:111
  116.4 14.1 %psum.15 = f32[1,512]{1,0:T(1,128)S(1)} all-reduce(f32[1,512]{1,0:T(1,128)S(1)} %psum.14), channel_id=1, replica_groups=mesh['face'=8,'sub'=4] {'face'}, use_global_device_ids=true, to_apply=%region_1.3 | all-reduce | flops 512 | bytes 4096 | tf_op jit(solution)/shard_map/psum | solution.py:112
  130.6 0.6 broadcast_multiply_fusion
  (11 shorter events, 0.0 us)
Async XLA Ops:
  7.2 47.0 %copy-start = (bf16[256,384]{1,0:T(8,128)(2,1)S(1)}, bf16[256,384]{1,0:T(8,128)(2,1)}, u32[]{:S(2)}) copy-start(bf16[256,384]{1,0:T(8,128)(2,1)} %param.19) | copy-start | bytes 589828
  7.2 36.3 %copy-start.3 = (bf16[1,128,512]{2,1,0:T(8,128)(2,1)S(1)}, bf16[1,128,512]{2,1,0:T(8,128)(2,1)}, u32[]{:S(2)}) copy-start(bf16[1,128,512]{2,1,0:T(8,128)(2,1)} %param.31) | copy-start | bytes 393220
  7.2 51.6 %all-gather.8.cloned.1.call-start = ((), (), s32[]{:S(2)}) async-start(), calls=%async_computation | async-start | bytes 1310720 | tf_op jit(solution)/shard_map/all_gather | solution.py:16
  7.9 82.2 %all-gather.10.cloned.1.call-start = ((), (), s32[]{:S(2)}) async-start(), calls=%async_computation.1 | async-start | bytes 1966080 | tf_op jit(solution)/shard_map/all_gather | solution.py:25
  8.7 96.6 %all-gather.12.cloned.1.call-start = ((), (), s32[]{:S(2)}) async-start(), calls=%async_computation.2 | async-start | bytes 1310720 | tf_op jit(solution)/shard_map/all_gather | solution.py:16
  54.6 2.0 %copy-start.1 = (bf16[256,512]{1,0:T(8,128)(2,1)S(1)}, bf16[256,512]{1,0:T(8,128)(2,1)}, u32[]{:S(2)}) copy-start(bf16[256,512]{1,0:T(8,128)(2,1)} %param.17) | copy-start | bytes 786436
  58.5 0.7 copy-start.6
  63.2 16.2 %collective-permute-start = (bf16[32,512]{1,0:T(8,128)(2,1)}, bf16[32,512]{1,0:T(8,128)(2,1)}, u32[]{:S(2)}, u32[]{:S(2)}) collective-permute-start(bf16[32,512]{1,0:T(8,128)(2,1)} %get-tuple-element.7), channel_id=1, source_target_pairs={{0,4},{4,8},{8,12},{12,16},{16,20},{20,24},{24,28},{28,0},{1,5},{5... | collective-permute-start | bytes 98312 | tf_op jit(solution)/shard_map/ppermute | solution.py:10
  63.2 17.0 %collective-permute-start.1 = (bf16[32,512]{1,0:T(8,128)(2,1)}, bf16[32,512]{1,0:T(8,128)(2,1)}, u32[]{:S(2)}, u32[]{:S(2)}) collective-permute-start(bf16[32,512]{1,0:T(8,128)(2,1)} %get-tuple-element.6), channel_id=1, source_target_pairs={{0,28},{4,0},{8,4},{12,8},{16,12},{20,16},{24,20},{28,24},{1,29},{... | collective-permute-start | bytes 98312 | tf_op jit(solution)/shard_map/ppermute | solution.py:10
  66.7 14.2 %collective-permute-start.2 = (bf16[32,512]{1,0:T(8,128)(2,1)}, bf16[32,512]{1,0:T(8,128)(2,1)S(1)}, u32[]{:S(2)}, u32[]{:S(2)}) collective-permute-start(bf16[32,512]{1,0:T(8,128)(2,1)} %get-tuple-element.5), channel_id=1, source_target_pairs={{0,1},{1,2},{2,3},{3,0},{4,5},{5,6},{6,7},{7,4},{8,9},{9,10},{10,1... | collective-permute-start | bytes 98312 | tf_op jit(solution)/shard_map/ppermute | solution.py:10
  67.1 13.8 %collective-permute-start.3 = (bf16[32,512]{1,0:T(8,128)(2,1)}, bf16[32,512]{1,0:T(8,128)(2,1)S(1)}, u32[]{:S(2)}, u32[]{:S(2)}) collective-permute-start(bf16[32,512]{1,0:T(8,128)(2,1)} %get-tuple-element.4), channel_id=1, source_target_pairs={{0,3},{1,0},{2,1},{3,2},{4,7},{5,4},{6,5},{7,6},{8,11},{9,8},{10,9... | collective-permute-start | bytes 98312 | tf_op jit(solution)/shard_map/ppermute | solution.py:10
  80.9 7.6 %copy-start.5 = (pred[2048]{0:T(1024)(128)(4,1)S(1)}, pred[2048]{0:T(1024)(128)(4,1)}, u32[]{:S(2)}) copy-start(pred[2048]{0:T(1024)(128)(4,1)} %compare_and_fusion.1) | copy-start | bytes 6148
  90.1 8.6 %copy-start.4 = (s32[2048]{0:T(1024)S(1)}, s32[2048]{0:T(1024)}, u32[]{:S(2)}) copy-start(s32[2048]{0:T(1024)} %param.21) | copy-start | bytes 24580
  98.7 8.6 %copy-start.8 = (bf16[2048,512]{1,0:T(8,128)(2,1)}, bf16[2048,512]{1,0:T(8,128)(2,1)S(1)}, u32[]{:S(2)}) copy-start(bf16[2048,512]{1,0:T(8,128)(2,1)S(1)} %add_convert_fusion) | copy-start | bytes 6291460
  100.5 6.8 %copy-start.7 = (f32[256]{0:T(256)S(1)}, f32[256]{0:T(256)}, u32[]{:S(2)}) copy-start(f32[256]{0:T(256)} %param.25) | copy-start | bytes 3076
  107.3 23.9 %copy-start.2 = (bf16[256,512]{1,0:T(8,128)(2,1)}, bf16[256,512]{1,0:T(8,128)(2,1)S(1)}, u32[]{:S(2)}) copy-start(bf16[256,512]{1,0:T(8,128)(2,1)S(1)} %fusion.10) | copy-start | bytes 786436
Sparse Core Ops, SparseCore 0:
  9.8 32.6 all-gather.7
  44.4 32.7 all-gather.9
  79.0 26.1 all-gather.11
